TPU v7x, 32 devices: a whole 2x2x4 slice. The times are simulated.
32 devices in a mesh: dp: 8 (over y, x, core), expert: 4 (over z).
Axes of the slice: x: 2, y: 2, z: 4, core: 2. Of those that a mesh axis runs over, the one named last changes fastest.
Arguments:
- tokens: bfloat16 [4096, 2048], P(('dp', 'expert')), may hold values from -6 to 6
- cotangent: bfloat16 [4096, 2048], P(('dp', 'expert')), may hold values from -6 to 6
- expert_ids: int32 [4096, 2], P(('dp', 'expert')), may hold values from 0 to 3, all different within a row; in each aligned block of 128 rows (0 to 127, 128 to 255, ...) at most 128 rows name the same one
- combine: float32 [4096, 2], P(('dp', 'expert')), may hold values from 0.1 to 1
- w_gate: bfloat16 [4, 2048, 768], P('expert'), may hold values from -0.125 to 0.125
- w_up: bfloat16 [4, 2048, 768], P('expert'), may hold values from -0.125 to 0.125
- w_down: bfloat16 [4, 768, 2048], P('expert'), may hold values from -0.21875 to 0.21875
Outputs:
- input_grad: bfloat16 [4096, 2048], P(('dp', 'expert'))
- combine_grad: float32 [4096, 2], P(('dp', 'expert'))
- gate_grad: bfloat16 [4, 2048, 768], P('expert', 'dp')
- up_grad: bfloat16 [4, 2048, 768], P('expert', 'dp')
- down_grad: bfloat16 [4, 768, 2048], P('expert', 'dp')
Inputs may be any that keep to these rules, and one draw needn't show every extreme that they name: `expert_ids`: each token names 2 different experts. In the rows of one device no expert is named by more than 128 tokens, and in some devices' rows some expert is named by exactly 128.
All inputs are finite; a program needn't handle non-finite values.
Results may differ from a plain program's by a relative error of at most 0.02.
Values may be sent and summed in bfloat16 or wider, within the bound.
A program may use at most 128 MiB of HBM per device.

v0:
```python
import jax
import jax.numpy as jnp
from jax import lax
from jax.sharding import PartitionSpec as P


def shards(tokens, cotangent, expert_ids, combine, w_gate, w_up, w_down):
    first = (((0,), (0,)), ((), ()))
    last = (((1,), (1,)), ((), ()))
    local = w_gate.shape[0]
    groups = lax.axis_size("expert")
    experts = local * groups
    rows, top = expert_ids.shape
    hidden_width = w_gate.shape[2]
    names = jnp.arange(experts, dtype=jnp.int32)
    hits = expert_ids[:, :, None] == names
    weight = jnp.sum(jnp.where(hits, combine[:, :, None], 0.0), axis=1)
    weight = lax.all_to_all(weight, "expert", split_axis=1, concat_axis=0, tiled=True)
    x = lax.all_gather(tokens, "expert", axis=0, tiled=True)
    dy = lax.all_gather(cotangent, "expert", axis=0, tiled=True)
    row_sum = 0.0
    combs, gates, ups, downs = ([], [], [], [])
    for i in range(local):
        w_g, w_u, w_d = (w_gate[i], w_up[i], w_down[i])
        gate = jnp.dot(x, w_g, preferred_element_type=jnp.float32)
        up = jnp.dot(x, w_u, preferred_element_type=jnp.float32)
        sig = jax.nn.sigmoid(gate)
        act = gate * sig
        hidden = (act * up).astype(jnp.bfloat16)
        scaled = (weight[:, i : i + 1] * dy.astype(jnp.float32)).astype(jnp.bfloat16)
        output = jnp.dot(hidden, w_d, preferred_element_type=jnp.float32)
        combs.append(jnp.sum(dy.astype(jnp.float32) * output, axis=1))
        hidden_grad = lax.dot_general(scaled, w_d, last, preferred_element_type=jnp.float32)
        gate_d = (hidden_grad * up * (sig * (1.0 + gate * (1.0 - sig)))).astype(jnp.bfloat16)
        up_d = (hidden_grad * act).astype(jnp.bfloat16)
        row = lax.dot_general(gate_d, w_g, last, preferred_element_type=jnp.float32)
        row = row + lax.dot_general(up_d, w_u, last, preferred_element_type=jnp.float32)
        row_sum = row_sum + row.astype(jnp.bfloat16).astype(jnp.float32)
        downs.append(lax.dot_general(hidden, scaled, first, preferred_element_type=jnp.float32))
        gates.append(lax.dot_general(x, gate_d, first, preferred_element_type=jnp.float32))
        ups.append(lax.dot_general(x, up_d, first, preferred_element_type=jnp.float32))

    def reduced(parts):
        return jnp.stack(
            [
                lax.psum_scatter(part.astype(jnp.bfloat16), "dp", scatter_dimension=0, tiled=True)
                for part in parts
            ]
        )

    down_grad = reduced(downs)
    gate_grad = reduced(gates)
    up_grad = reduced(ups)
    input_grad = lax.psum_scatter(
        row_sum.astype(jnp.bfloat16), "expert", scatter_dimension=0, tiled=True
    )
    comb = jnp.stack(combs)
    comb = lax.all_to_all(comb, "expert", split_axis=1, concat_axis=0, tiled=True)
    combine_grad = jnp.sum(jnp.where(hits, comb.T[:, None, :], 0.0), axis=2)
    return (input_grad, combine_grad, gate_grad, up_grad, down_grad)


def solution(mesh):
    by_token = P(("dp", "expert"), None)
    by_expert = P("expert", None, None)
    by_row = P("expert", "dp", None)
    return jax.shard_map(
        shards,
        mesh=mesh,
        in_specs=(by_token,) * 4 + (by_expert,) * 3,
        out_specs=(by_token, by_token, by_row, by_row, by_row),
        check_vma=False,
    )
```

profile of v0, /device:TPU:0, one launch (start us, length us, event | category | flops | bytes accessed | tf_op | source)
XLA Modules:
  0.0 329.0 jit_solution(15756444999730954706)
XLA Ops:
  7.2 0.0 all-gather.5.cloned.1.call-start
  7.2 0.7 all-gather.5.cloned.1.call-update
  7.9 0.0 all-gather.3.cloned.1.call-start
  8.0 0.7 all-gather.3.cloned.1.call-update
  8.7 0.0 reduce-scatter.9.cloned.1.call-start
  8.7 49.3 %all-gather.5.cloned.1.call-done = bf16[512,2048]{1,0:T(8,128)(2,1)} async-done(((bf16[128,2048]{1,0:T(8,128)(2,1)}), bf16[512,2048]{1,0:T(8,128)(2,1)}) %all-gather.5.cloned.1.call-update) | async-done | bytes 2097168 | tf_op jit(solution)/shard_map/all_gather | solution.py:19
  58.0 4.5 %fusion.4 = f32[512,768]{1,0:T(8,128)S(1)} fusion(bf16[512,2048]{1,0:T(8,128)(2,1)} %all-gather.5.cloned.1.call-done, bf16[1,2048,768]{2,1,0:T(8,128)(2,1)} %param.11), kind=kOutput, calls=%fused_computation.10 | convolution fusion | flops 1610612736 | bytes 6815744 | tf_op jit(solution)/shard_map/dot_general | solution.py:25
  62.4 1.2 copy-done.9
  63.6 3.2 multiply_convert_fusion
  66.9 37.2 %all-gather.3.cloned.1.call-done = bf16[512,2048]{1,0:T(8,128)(2,1)} async-done(((bf16[128,2048]{1,0:T(8,128)(2,1)}), bf16[512,2048]{1,0:T(8,128)(2,1)}) %all-gather.3.cloned.1.call-update) | async-done | bytes 2097168 | tf_op jit(solution)/shard_map/all_gather | solution.py:20
  104.1 4.8 %fusion.1 = f32[512]{0:T(512)S(1)} fusion(bf16[512,2048]{1,0:T(8,128)(2,1)} %all-gather.3.cloned.1.call-done, bf16[512,768]{1,0:T(8,128)(2,1)} %get-tuple-element.29, bf16[1,768,2048]{2,1,0:T(8,128)(2,1)} %param.13), kind=kOutput, calls=%fused_computation.3 | convolution fusion | flops 1613757952 | bytes 6031360 | tf_op jit(solution)/shard_map/dot_general | solution.py:31
  108.9 8.0 %all_to_all.32 = f32[1,4,128]{2,0,1:T(1,128)S(1)} all-to-all(f32[1,4,128]{2,0,1:T(1,128)S(1)} %bitcast.56), channel_id=1, replica_groups=mesh['dp'=8,'expert'=4] {'expert'}, dimensions={1} | all-to-all | bytes 4096 | tf_op jit(solution)/shard_map/all_to_all | solution.py:58
  116.9 0.6 select_reduce_fusion
  117.5 7.9 %all_to_all.33 = f32[128,4,1]{0,2,1:T(1,128)S(1)} all-to-all(f32[128,4,1]{0,2,1:T(1,128)S(1)} %bitcast.53), channel_id=1, replica_groups=mesh['dp'=8,'expert'=4] {'expert'}, dimensions={1} | all-to-all | bytes 4096 | tf_op jit(solution)/shard_map/all_to_all | solution.py:18
  125.4 3.3 multiply_convert_fusion.1
  128.7 0.9 copy-done.7
  129.6 3.5 %fusion.14 = bf16[2048,768]{0,1:T(8,128)(2,1)} fusion(bf16[512,768]{1,0:T(8,128)(2,1)S(1)} %get-tuple-element.27, bf16[512,2048]{1,0:T(8,128)(2,1)S(1)} %copy-done.6), kind=kOutput, calls=%fused_computation.20 | convolution fusion | flops 1612185600 | bytes 6029312 | tf_op jit(solution)/shard_map/dot_general | solution.py:41
  133.1 0.0 reduce-scatter.7.cloned.1.call-start
  133.2 5.3 %fusion.13 = bf16[2048,768]{0,1:T(8,128)(2,1)} fusion(bf16[512,768]{1,0:T(8,128)(2,1)} %get-tuple-element.28, bf16[512,2048]{1,0:T(8,128)(2,1)} %all-gather.5.cloned.1.call-done), kind=kOutput, calls=%fused_computation.19 | convolution fusion | flops 1612185600 | bytes 6029312 | tf_op jit(solution)/shard_map/dot_general | solution.py:40
  138.5 0.0 reduce-scatter.7.cloned.1.call-update
  138.5 0.2 reduce-scatter.5.cloned.1.call-start
  138.7 4.3 %fusion.2 = f32[512,2048]{1,0:T(8,128)S(1)} fusion(bf16[512,768]{1,0:T(8,128)(2,1)} %get-tuple-element.28, bf16[1,2048,768]{2,1,0:T(8,128)(2,1)} %param.11), kind=kOutput, calls=%fused_computation.8 | convolution fusion | flops 1610612736 | bytes 8126464 | tf_op jit(solution)/shard_map/dot_general | solution.py:36
  143.1 3.3 add_convert_fusion
  146.3 0.0 reduce-scatter.5.cloned.1.call-update
  146.4 0.0 reduce-scatter.11.cloned.1.call-start
  146.4 5.5 %convolution_convert_fusion = bf16[768,2048]{1,0:T(8,128)(2,1)} fusion(bf16[512,768]{1,0:T(8,128)(2,1)} %get-tuple-element.29, bf16[512,2048]{1,0:T(8,128)(2,1)} %all-gather.3.cloned.1.call-done, f32[512]{0:T(512)S(1)} %bitcast.55), kind=kOutput, calls=%fused_computation.5 | convolution fusion | flops 1615331328 | bytes 6031360 | tf_op jit(solution)/shard_map/dot_general | solution.py:39
  151.9 25.5 %reduce-scatter.9.cloned.1.call-done = bf16[256,768]{0,1:T(8,128)(2,1)} async-done(((bf16[2048,768]{0,1:T(8,128)(2,1)}), bf16[256,768]{0,1:T(8,128)(2,1)}) %reduce-scatter.9.cloned.1.call-update) | async-done | bytes 393232 | tf_op jit(solution)/shard_map/reduce_scatter | solution.py:46
  177.4 1.9 copy.30
  179.3 47.4 %reduce-scatter.7.cloned.1.call-done = bf16[256,768]{0,1:T(8,128)(2,1)} async-done(((bf16[2048,768]{0,1:T(8,128)(2,1)}), bf16[256,768]{0,1:T(8,128)(2,1)}) %reduce-scatter.7.cloned.1.call-update) | async-done | bytes 393232 | tf_op jit(solution)/shard_map/reduce_scatter | solution.py:46
  226.7 1.9 copy.29
  228.6 44.4 %reduce-scatter.5.cloned.1.call-done = bf16[128,2048]{1,0:T(8,128)(2,1)} async-done(((bf16[512,2048]{1,0:T(8,128)(2,1)}), bf16[128,2048]{1,0:T(8,128)(2,1)}) %reduce-scatter.5.cloned.1.call-update) | async-done | bytes 524304 | tf_op jit(solution)/shard_map/reduce_scatter | solution.py:54
  273.0 49.1 %reduce-scatter.11.cloned.1.call-done = bf16[96,2048]{1,0:T(8,128)(2,1)} async-done(((bf16[768,2048]{1,0:T(8,128)(2,1)}), bf16[96,2048]{1,0:T(8,128)(2,1)}) %reduce-scatter.11.cloned.1.call-update) | async-done | bytes 393232 | tf_op jit(solution)/shard_map/reduce_scatter | solution.py:46
  (24 shorter events, 0.1 us)
Async XLA Ops:
  7.2 56.4 %copy-start = (bf16[1,2048,768]{2,1,0:T(8,128)(2,1)S(1)}, bf16[1,2048,768]{2,1,0:T(8,128)(2,1)}, u32[]{:S(2)}) copy-start(bf16[1,2048,768]{2,1,0:T(8,128)(2,1)} %param.12) | copy-start | bytes 9437188
  7.2 50.8 %all-gather.5.cloned.1.call-start = ((), (), s32[]{:S(2)}) async-start(), calls=%async_computation.7 | async-start | bytes 2621440 | tf_op jit(solution)/shard_map/all_gather | solution.py:19
  7.9 96.1 %all-gather.3.cloned.1.call-start = ((), (), s32[]{:S(2)}) async-start(), calls=%async_computation.6 | async-start | bytes 2621440 | tf_op jit(solution)/shard_map/all_gather | solution.py:20
  8.7 168.7 %reduce-scatter.9.cloned.1.call-start = ((), (), s32[]{:S(2)}) async-start(), calls=%async_computation.10 | async-start | bytes 3538944 | tf_op jit(solution)/shard_map/reduce_scatter | solution.py:46
  58.0 5.6 %copy-start.5 = (bf16[512,2048]{1,0:T(8,128)(2,1)S(1)}, bf16[512,2048]{1,0:T(8,128)(2,1)}, u32[]{:S(2)}) copy-start(bf16[512,2048]{1,0:T(8,128)(2,1)} %all-gather.5.cloned.1.call-done) | copy-start | bytes 6291460
  62.4 1.2 copy-start.9
  104.0 12.9 %copy-start.1 = (s32[128,2]{0,1:T(2,128)S(1)}, s32[128,2]{0,1:T(2,128)}, u32[]{:S(2)}) copy-start(s32[128,2]{0,1:T(2,128)} %param.9) | copy-start | bytes 3076
  104.0 12.9 %copy-start.2 = (f32[128,2]{0,1:T(2,128)S(1)}, f32[128,2]{0,1:T(2,128)}, u32[]{:S(2)}) copy-start(f32[128,2]{0,1:T(2,128)} %param.10) | copy-start | bytes 3076
  104.0 21.3 %copy-start.3 = (bf16[1,768,2048]{2,1,0:T(8,128)(2,1)S(1)}, bf16[1,768,2048]{2,1,0:T(8,128)(2,1)}, u32[]{:S(2)}) copy-start(bf16[1,768,2048]{2,1,0:T(8,128)(2,1)} %param.13) | copy-start | bytes 9437188
  104.0 21.3 %copy-start.4 = (bf16[512,2048]{1,0:T(8,128)(2,1)S(1)}, bf16[512,2048]{1,0:T(8,128)(2,1)}, u32[]{:S(2)}) copy-start(bf16[512,2048]{1,0:T(8,128)(2,1)} %all-gather.3.cloned.1.call-done) | copy-start | bytes 6291460
  104.0 21.3 %copy-start.10 = (f32[512,768]{1,0:T(8,128)S(1)}, f32[512,768]{1,0:T(8,128)}, u32[]{:S(2)}) copy-start(f32[512,768]{1,0:T(8,128)} %copy-done.9) | copy-start | bytes 4718596
  104.0 21.3 %copy-start.11 = (f32[512,768]{1,0:T(8,128)S(1)}, f32[512,768]{1,0:T(8,128)}, u32[]{:S(2)}) copy-start(f32[512,768]{1,0:T(8,128)} %get-tuple-element.30) | copy-start | bytes 4718596
  125.4 4.2 %copy-start.6 = (bf16[512,2048]{1,0:T(8,128)(2,1)S(1)}, bf16[512,2048]{1,0:T(8,128)(2,1)}, u32[]{:S(2)}) copy-start(bf16[512,2048]{1,0:T(8,128)(2,1)} %all-gather.5.cloned.1.call-done) | copy-start | bytes 6291460
  128.7 0.9 copy-start.7
  133.1 93.6 %reduce-scatter.7.cloned.1.call-start = ((), (), s32[]{:S(2)}) async-start(), calls=%async_computation.9 | async-start | bytes 3538944 | tf_op jit(solution)/shard_map/reduce_scatter | solution.py:46
  138.5 134.5 %reduce-scatter.5.cloned.1.call-start = ((), (), s32[]{:S(2)}) async-start(), calls=%async_computation.8 | async-start | bytes 2621440 | tf_op jit(solution)/shard_map/reduce_scatter | solution.py:54
  138.7 4.3 %copy-start.8 = (bf16[512,768]{1,0:T(8,128)(2,1)S(1)}, bf16[512,768]{1,0:T(8,128)(2,1)}, u32[]{:S(2)}) copy-start(bf16[512,768]{1,0:T(8,128)(2,1)} %copy-done.7) | copy-start | bytes 2359300
  146.4 175.8 %reduce-scatter.11.cloned.1.call-start = ((), (), s32[]{:S(2)}) async-start(), calls=%async_computation.11 | async-start | bytes 3538944 | tf_op jit(solution)/shard_map/reduce_scatter | solution.py:46
Sparse Core Ops, SparseCore 0:
  9.6 48.3 all-gather.4
  59.5 44.4 all-gather.2
  133.2 44.0 reduce-scatter.8
  180.6 46.0 reduce-scatter.6
  229.4 43.5 reduce-scatter.4
  276.8 45.2 reduce-scatter.10
where the time goes:
time: 329 us
  waiting for transfers between devices  254 us (77%)
  matrix products  37.7 us (11%)
  blocking collectives  15.9 us (5%)
  between operations  14.2 us (4%)
  local copies, waits for them, and re-layouts  5.92 us (2%)
    reduce_scatter x3, waiting for transfers between devices, reduced(): lax.psum_scatter(part.astype(jnp.bfloat16), 'dp', scatter_dimension=0, ti...  122 us
    all_gather x1, waiting for transfers between devices, shards(): x = lax.all_gather(tokens, 'expert', axis=0, tiled=True)  49.3 us
    reduce_scatter x1, waiting for transfers between devices, shards(): lax.psum_scatter(row_sum.astype(jnp.bfloat16), 'expert', scatter_dimensio...  44.4 us
    all_gather x1, waiting for transfers between devices, shards(): dy = lax.all_gather(cotangent, 'expert', axis=0, tiled=True)  37.2 us
    all_to_all x1, blocking collectives, shards(): lax.all_to_all(comb, 'expert', split_axis=1, concat_axis=0, tiled=True)  8.03 us
    all_to_all x1, blocking collectives, shards(): lax.all_to_all(weight, 'expert', split_axis=1, concat_axis=0, tiled=True)  7.9 us
  transfers between devices with their start and end apart: 6, of which 6 were waited for; matrix products, arithmetic and copies ran while one was open for 9% of the time, Pallas kernels for 0%

commit v1 on v0

--- a/solution.py
+++ b/solution.py
@@ -16,7 +16,14 @@
     hits = expert_ids[:, :, None] == names
     weight = jnp.sum(jnp.where(hits, combine[:, :, None], 0.0), axis=1)
     weight = lax.all_to_all(weight, "expert", split_axis=1, concat_axis=0, tiled=True)
-    x = lax.all_gather(tokens, "expert", axis=0, tiled=True)
+    ring = [tokens]
+    for hop in range(3):
+        ring.append(lax.ppermute(ring[-1], "expert", [(dev, (dev + 1) % 4) for dev in range(4)]))
+    x = jnp.roll(
+        jnp.concatenate(ring[::-1], axis=0),
+        (lax.axis_index("expert") + 1) * ring[0].shape[0],
+        axis=0,
+    )
     dy = lax.all_gather(cotangent, "expert", axis=0, tiled=True)
     row_sum = 0.0
     combs, gates, ups, downs = ([], [], [], [])

time: 329 us -> 315 us (0.957)
  waiting for transfers between devices: 254 us -> 240 us
  matrix products: 37.7 us -> 33.3 us
    all_gather x1 -> x0, waiting for transfers between devices: 49.3 us -> none  [shards(): x = lax.all_gather(tokens, 'expert', axis=0, tiled=True)]
    ppermute x0 -> x3, waiting for transfers between devices: none -> 44.6 us  [shards(): lax.ppermute(ring[-1], 'expert', [(dev, (dev + 1) % 4) for dev in range(4)])]
    reduce_scatter x3, waiting for transfers between devices: 122 us -> 149 us  [reduced(): lax.psum_scatter(part.astype(jnp.bfloat16), 'dp', scatter_dimension=0, ti...]
    reduce_scatter x1, waiting for transfers between devices: 44.4 us -> 25.1 us  [shards(): lax.psum_scatter(row_sum.astype(jnp.bfloat16), 'expert', scatter_dimensio...]
    all_gather x1, waiting for transfers between devices: 37.2 us -> 21.1 us  [shards(): dy = lax.all_gather(cotangent, 'expert', axis=0, tiled=True)]
    unnamed x26 -> x39, local copies, waits for them, and re-layouts: 5.92 us -> 7.82 us
  transfers between devices with their start and end apart: 6 -> 8, of which waited for: 6 -> 8; matrix products, arithmetic and copies ran while one was open for 9% -> 9% of each run, Pallas kernels for 0% -> 0%
where the time goes in v1:
time: 315 us
  waiting for transfers between devices  240 us (76%)
  matrix products  33.3 us (11%)
  blocking collectives  15.8 us (5%)
  between operations  14 us (4%)
  local copies, waits for them, and re-layouts  7.85 us (2%)
  starting transfers between devices  3.49 us (1%)
    reduce_scatter x3, waiting for transfers between devices, reduced(): lax.psum_scatter(part.astype(jnp.bfloat16), 'dp', scatter_dimension=0, ti...  149 us
    ppermute x3, waiting for transfers between devices, shards(): lax.ppermute(ring[-1], 'expert', [(dev, (dev + 1) % 4) for dev in range(4)])  44.6 us
    reduce_scatter x1, waiting for transfers between devices, shards(): lax.psum_scatter(row_sum.astype(jnp.bfloat16), 'expert', scatter_dimensio...  25.1 us
    all_gather x1, waiting for transfers between devices, shards(): dy = lax.all_gather(cotangent, 'expert', axis=0, tiled=True)  21.1 us
    all_to_all x1, blocking collectives, shards(): lax.all_to_all(comb, 'expert', split_axis=1, concat_axis=0, tiled=True)  7.91 us
    all_to_all x1, blocking collectives, shards(): lax.all_to_all(weight, 'expert', split_axis=1, concat_axis=0, tiled=True)  7.9 us
    unnamed x39, local copies, waits for them, and re-layouts  7.82 us
  transfers between devices with their start and end apart: 8, of which 8 were waited for; matrix products, arithmetic and copies ran while one was open for 9% of the time, Pallas kernels for 0%

profile of v1, /device:TPU:0, one launch (start us, length us, event | category | flops | bytes accessed | tf_op | source)
XLA Modules:
  0.0 314.8 jit_solution(17597864913126749833)
XLA Ops:
  7.2 3.1 collective-permute-start
  10.3 14.2 %collective-permute-done = bf16[128,2048]{1,0:T(8,128)(2,1)S(1)} collective-permute-done((bf16[128,2048]{1,0:T(8,128)(2,1)}, bf16[128,2048]{1,0:T(8,128)(2,1)S(1)}, u32[]{:S(2)}, u32[]{:S(2)}) %collective-permute-start) | collective-permute-done | bytes 524320 | tf_op jit(solution)/shard_map/ppermute | solution.py:21
  24.5 0.8 copy-done.2
  25.3 15.0 %collective-permute-done.1 = bf16[128,2048]{1,0:T(8,128)(2,1)} collective-permute-done((bf16[128,2048]{1,0:T(8,128)(2,1)S(1)}, bf16[128,2048]{1,0:T(8,128)(2,1)}, u32[]{:S(2)}, u32[]{:S(2)}) %collective-permute-start.1) | collective-permute-done | bytes 524320 | tf_op jit(solution)/shard_map/ppermute | solution.py:21
  40.3 0.0 reduce-scatter.5.cloned.1.call-start
  40.4 15.4 %collective-permute-done.2 = bf16[128,2048]{1,0:T(8,128)(2,1)} collective-permute-done((bf16[128,2048]{1,0:T(8,128)(2,1)}, bf16[128,2048]{1,0:T(8,128)(2,1)}, u32[]{:S(2)}, u32[]{:S(2)}) %collective-permute-start.2) | collective-permute-done | bytes 524320 | tf_op jit(solution)/shard_map/ppermute | solution.py:21
  55.8 1.1 constant_dynamic-update-slice_fusion.7
  56.9 1.1 constant_dynamic-update-slice_fusion.6
  58.0 1.2 constant_dynamic-update-slice_fusion.5
  59.3 1.1 constant_dynamic-update-slice_fusion.3
  60.4 1.1 constant_dynamic-update-slice_fusion.2
  61.6 1.8 fusion.4
  63.4 0.2 copy-done.4
  63.5 1.2 copy-done.13
  64.7 3.3 %multiply_convert_fusion = (bf16[512,768]{1,0:T(8,128)(2,1)}, f32[512,768]{1,0:T(8,128)}) fusion(f32[512,768]{1,0:T(8,128)S(1)} %fusion.4, bf16[1,2048,768]{2,1,0:T(8,128)(2,1)S(1)} %copy-done, bf16[1024,2048]{1,0:T(8,128)(2,1)S(1)} %constant_dynamic-update-slice_fusion, s32[]{:T(128)S(6)} %select_n.23), kind=kOutput, calls=%fused_computation.19 | convolution fusion | flops 1612972032 | bytes 9175044 | tf_op jit(solution)/shard_map/dot_general | solution.py:33
  68.0 21.1 %all-gather.2.cloned.1.call-done = bf16[512,2048]{1,0:T(8,128)(2,1)} async-done(((bf16[128,2048]{1,0:T(8,128)(2,1)}), bf16[512,2048]{1,0:T(8,128)(2,1)}) %all-gather.2.cloned.1.call-update) | async-done | bytes 2097168 | tf_op jit(solution)/shard_map/all_gather | solution.py:27
  89.1 4.8 %fusion.1 = f32[512]{0:T(512)S(1)} fusion(bf16[512,2048]{1,0:T(8,128)(2,1)} %all-gather.2.cloned.1.call-done, bf16[512,768]{1,0:T(8,128)(2,1)} %get-tuple-element.9, bf16[1,768,2048]{2,1,0:T(8,128)(2,1)} %param.13), kind=kOutput, calls=%fused_computation.3 | convolution fusion | flops 1613757952 | bytes 6031360 | tf_op jit(solution)/shard_map/dot_general | solution.py:38
  93.9 7.9 %all_to_all.32 = f32[1,4,128]{2,0,1:T(1,128)S(1)} all-to-all(f32[1,4,128]{2,0,1:T(1,128)S(1)} %bitcast.46), channel_id=1, replica_groups=mesh['dp'=8,'expert'=4] {'expert'}, dimensions={1} | all-to-all | bytes 4096 | tf_op jit(solution)/shard_map/all_to_all | solution.py:65
  101.8 0.6 select_reduce_fusion
  102.4 7.9 %all_to_all.33 = f32[128,4,1]{0,2,1:T(1,128)S(1)} all-to-all(f32[128,4,1]{0,2,1:T(1,128)S(1)} %bitcast.43), channel_id=1, replica_groups=mesh['dp'=8,'expert'=4] {'expert'}, dimensions={1} | all-to-all | bytes 4096 | tf_op jit(solution)/shard_map/all_to_all | solution.py:18
  110.3 2.3 multiply_convert_fusion.1
  112.7 1.8 fusion.2
  114.5 3.1 add_convert_fusion
  117.7 0.0 reduce-scatter.11.cloned.1.call-start
  117.7 5.4 %convolution_convert_fusion = bf16[768,2048]{1,0:T(8,128)(2,1)} fusion(bf16[512,768]{1,0:T(8,128)(2,1)} %get-tuple-element.9, bf16[512,2048]{1,0:T(8,128)(2,1)} %all-gather.2.cloned.1.call-done, f32[512]{0:T(512)S(1)} %bitcast.45), kind=kOutput, calls=%fused_computation.5 | convolution fusion | flops 1615331328 | bytes 6031360 | tf_op jit(solution)/shard_map/dot_general | solution.py:46
  123.2 0.2 reduce-scatter.7.cloned.1.call-start
  123.4 5.3 %convolution_convert_fusion.2 = bf16[2048,768]{1,0:T(8,128)(2,1)} fusion(bf16[512,768]{1,0:T(8,128)(2,1)} %copy-done.12, bf16[1024,2048]{1,0:T(8,128)(2,1)} %copy-done.4, s32[]{:T(128)S(6)} %select_n.23), kind=kOutput, calls=%fused_computation.7 | convolution fusion | flops 1612185600 | bytes 6029316 | tf_op jit(solution)/shard_map/dot_general | solution.py:47
  128.8 5.4 %convolution_convert_fusion.1 = bf16[2048,768]{1,0:T(8,128)(2,1)} fusion(bf16[512,768]{1,0:T(8,128)(2,1)} %copy-done.11, bf16[1024,2048]{1,0:T(8,128)(2,1)} %copy-done.4, s32[]{:T(128)S(6)} %select_n.23), kind=kOutput, calls=%fused_computation.6 | convolution fusion | flops 1612185600 | bytes 6029316 | tf_op jit(solution)/shard_map/dot_general | solution.py:48
  134.2 25.1 %reduce-scatter.5.cloned.1.call-done = bf16[128,2048]{1,0:T(8,128)(2,1)} async-done(((bf16[512,2048]{1,0:T(8,128)(2,1)}), bf16[128,2048]{1,0:T(8,128)(2,1)}) %reduce-scatter.5.cloned.1.call-update) | async-done | bytes 524304 | tf_op jit(solution)/shard_map/reduce_scatter | solution.py:61
  159.3 49.3 %reduce-scatter.11.cloned.1.call-done = bf16[96,2048]{1,0:T(8,128)(2,1)} async-done(((bf16[768,2048]{1,0:T(8,128)(2,1)}), bf16[96,2048]{1,0:T(8,128)(2,1)}) %reduce-scatter.11.cloned.1.call-update) | async-done | bytes 393232 | tf_op jit(solution)/shard_map/reduce_scatter | solution.py:53
  208.5 49.9 %reduce-scatter.7.cloned.1.call-done = bf16[256,768]{1,0:T(8,128)(2,1)} async-done(((bf16[2048,768]{1,0:T(8,128)(2,1)}), bf16[256,768]{1,0:T(8,128)(2,1)}) %reduce-scatter.7.cloned.1.call-update) | async-done | bytes 393232 | tf_op jit(solution)/shard_map/reduce_scatter | solution.py:53
  258.4 49.9 %reduce-scatter.9.cloned.1.call-done = bf16[256,768]{1,0:T(8,128)(2,1)} async-done(((bf16[2048,768]{1,0:T(8,128)(2,1)}), bf16[256,768]{1,0:T(8,128)(2,1)}) %reduce-scatter.9.cloned.1.call-update) | async-done | bytes 393232 | tf_op jit(solution)/shard_map/reduce_scatter | solution.py:53
  (41 shorter events, 0.3 us)
Async XLA Ops:
  7.2 57.5 %copy-start = (bf16[1,2048,768]{2,1,0:T(8,128)(2,1)S(1)}, bf16[1,2048,768]{2,1,0:T(8,128)(2,1)}, u32[]{:S(2)}) copy-start(bf16[1,2048,768]{2,1,0:T(8,128)(2,1)} %param.12) | copy-start | bytes 9437188
  7.2 81.9 %all-gather.2.cloned.1.call-start = ((), (), s32[]{:S(2)}) async-start(), calls=%async_computation.6 | async-start | bytes 2621440 | tf_op jit(solution)/shard_map/all_gather | solution.py:27
  7.2 17.3 %collective-permute-start = (bf16[128,2048]{1,0:T(8,128)(2,1)}, bf16[128,2048]{1,0:T(8,128)(2,1)S(1)}, u32[]{:S(2)}, u32[]{:S(2)}) collective-permute-start(bf16[128,2048]{1,0:T(8,128)(2,1)} %param.7), channel_id=1, source_target_pairs={{0,1},{1,2},{2,3},{3,0},{4,5},{5,6},{6,7},{7,4},{8,9},{9,10},{10,1... | collective-permute-start | bytes 1572872 | tf_op jit(solution)/shard_map/ppermute | solution.py:21
  24.5 0.8 copy-start.2
  25.3 15.0 %collective-permute-start.1 = (bf16[128,2048]{1,0:T(8,128)(2,1)S(1)}, bf16[128,2048]{1,0:T(8,128)(2,1)}, u32[]{:S(2)}, u32[]{:S(2)}) collective-permute-start(bf16[128,2048]{1,0:T(8,128)(2,1)S(1)} %collective-permute-done), channel_id=1, source_target_pairs={{0,1},{1,2},{2,3},{3,0},{4,5},{5,6},{6,7},{7,4},{8,9},{9,10},{10,1... | collective-permute-start | bytes 1572872 | tf_op jit(solution)/shard_map/ppermute | solution.py:21
  40.3 15.5 %collective-permute-start.2 = (bf16[128,2048]{1,0:T(8,128)(2,1)}, bf16[128,2048]{1,0:T(8,128)(2,1)}, u32[]{:S(2)}, u32[]{:S(2)}) collective-permute-start(bf16[128,2048]{1,0:T(8,128)(2,1)} %collective-permute-done.1), channel_id=1, source_target_pairs={{0,1},{1,2},{2,3},{3,0},{4,5},{5,6},{6,7},{7,4},{8,9},{9,10},{10,1... | collective-permute-start | bytes 1572872 | tf_op jit(solution)/shard_map/ppermute | solution.py:21
  40.3 119.0 %reduce-scatter.5.cloned.1.call-start = ((), (), s32[]{:S(2)}) async-start(), calls=%async_computation.7 | async-start | bytes 2621440 | tf_op jit(solution)/shard_map/reduce_scatter | solution.py:61
  40.4 18.9 %copy-start.1 = (bf16[128,2048]{1,0:T(8,128)(2,1)S(1)}, bf16[128,2048]{1,0:T(8,128)(2,1)}, u32[]{:S(2)}) copy-start(bf16[128,2048]{1,0:T(8,128)(2,1)} %param.7) | copy-start | bytes 1572868
  40.4 21.1 %copy-start.3 = (bf16[128,2048]{1,0:T(8,128)(2,1)S(1)}, bf16[128,2048]{1,0:T(8,128)(2,1)}, u32[]{:S(2)}) copy-start(bf16[128,2048]{1,0:T(8,128)(2,1)} %copy-done.2) | copy-start | bytes 1572868
  58.0 3.6 %copy-start.8 = (bf16[1,2048,768]{2,1,0:T(8,128)(2,1)S(1)}, bf16[1,2048,768]{2,1,0:T(8,128)(2,1)}, u32[]{:S(2)}) copy-start(bf16[1,2048,768]{2,1,0:T(8,128)(2,1)} %param.11) | copy-start | bytes 9437188
  61.6 2.0 copy-start.4
  63.5 1.2 copy-start.13
  89.0 12.7 %copy-start.5 = (s32[128,2]{0,1:T(2,128)S(1)}, s32[128,2]{0,1:T(2,128)}, u32[]{:S(2)}) copy-start(s32[128,2]{0,1:T(2,128)} %param.9) | copy-start | bytes 3076
  89.0 12.7 %copy-start.6 = (f32[128,2]{0,1:T(2,128)S(1)}, f32[128,2]{0,1:T(2,128)}, u32[]{:S(2)}) copy-start(f32[128,2]{0,1:T(2,128)} %param.10) | copy-start | bytes 3076
  89.1 21.2 %copy-start.7 = (bf16[1,768,2048]{2,1,0:T(8,128)(2,1)S(1)}, bf16[1,768,2048]{2,1,0:T(8,128)(2,1)}, u32[]{:S(2)}) copy-start(bf16[1,768,2048]{2,1,0:T(8,128)(2,1)} %param.13) | copy-start | bytes 9437188
  89.1 21.2 %copy-start.10 = (bf16[512,2048]{1,0:T(8,128)(2,1)S(1)}, bf16[512,2048]{1,0:T(8,128)(2,1)}, u32[]{:S(2)}) copy-start(bf16[512,2048]{1,0:T(8,128)(2,1)} %all-gather.2.cloned.1.call-done) | copy-start | bytes 6291460
  89.1 21.2 %copy-start.14 = (f32[512,768]{1,0:T(8,128)S(1)}, f32[512,768]{1,0:T(8,128)}, u32[]{:S(2)}) copy-start(f32[512,768]{1,0:T(8,128)} %copy-done.13) | copy-start | bytes 4718596
  89.1 21.2 %copy-start.15 = (f32[512,768]{1,0:T(8,128)S(1)}, f32[512,768]{1,0:T(8,128)}, u32[]{:S(2)}) copy-start(f32[512,768]{1,0:T(8,128)} %get-tuple-element.10) | copy-start | bytes 4718596
  110.3 2.4 copy-start.9
  112.6 1.9 copy-start.12
  112.7 1.9 copy-start.11
  117.7 90.9 %reduce-scatter.11.cloned.1.call-start = ((), (), s32[]{:S(2)}) async-start(), calls=%async_computation.10 | async-start | bytes 3538944 | tf_op jit(solution)/shard_map/reduce_scatter | solution.py:53
  123.2 135.2 %reduce-scatter.7.cloned.1.call-start = ((), (), s32[]{:S(2)}) async-start(), calls=%async_computation.8 | async-start | bytes 3538944 | tf_op jit(solution)/shard_map/reduce_scatter | solution.py:53
  128.8 179.5 %reduce-scatter.9.cloned.1.call-start = ((), (), s32[]{:S(2)}) async-start(), calls=%async_computation.9 | async-start | bytes 3538944 | tf_op jit(solution)/shard_map/reduce_scatter | solution.py:53
Sparse Core Ops, SparseCore 0:
  40.4 48.5 all-gather.1
  117.8 41.4 reduce-scatter.4
  163.2 45.2 reduce-scatter.10
  212.4 46.0 reduce-scatter.6
  262.2 46.0 reduce-scatter.8
